TPU v7x, 32 devices: a 4x4x1 block of a 4x4x8 slice. The times are simulated.
32 devices in a mesh: dp: 1 (over z), tp: 4 (over y), cp: 8 (over x, core).
Axes of the slice: x: 4, y: 4, z: 1, core: 2. Of those that a mesh axis runs over, the one named last changes fastest.
The devices are a block of a 4x4x8 slice.
Arguments:
- x: bfloat16 [4096, 5120], P(('dp', 'cp'))
- doc_ids: int32 [4096], P(('dp', 'cp'))
- w_query: bfloat16 [5120, 4096], P(None, 'tp')
- w_key: bfloat16 [5120, 1024], P(None, 'tp')
- w_value: bfloat16 [5120, 1024], P(None, 'tp')
- w_out: bfloat16 [4096, 5120], P('tp')
Outputs:
- output: bfloat16 [4096, 5120], P(('dp', 'cp'))
All inputs are finite; a program needn't handle non-finite values.
Results may differ from a plain program's by a relative error of at most 0.00717162.
Values are sent between devices in bfloat16 or wider.
A program may use at most 768 MiB of HBM per device.

v0:
```python
import jax
import jax.numpy as jnp
from jax import lax
from jax.sharding import PartitionSpec as P

HEAD_DIM = 128


def block_update(soft_state, q_blk, k_blk, v_blk, allowed):
    run_max, run_sum, out_acc = soft_state
    scores = jnp.einsum('qhgd,khd->qhgk', q_blk, k_blk, preferred_element_type=jnp.float32) * (HEAD_DIM ** -0.5)
    scores = jnp.where(allowed[:, None, None, :], scores, -jnp.inf)
    new_max = jnp.maximum(run_max, jnp.max(scores, axis=-1))
    safe_max = jnp.where(new_max == -jnp.inf, 0.0, new_max)
    prob_vals = jnp.exp(scores - safe_max[..., None])
    rescale = jnp.exp(run_max - safe_max)
    run_sum = run_sum * rescale + jnp.sum(prob_vals, axis=-1)
    out_acc = out_acc * rescale[..., None] + jnp.einsum('qhgk,khd->qhgd', prob_vals.astype(jnp.bfloat16), v_blk, preferred_element_type=jnp.float32)
    return new_max, run_sum, out_acc


def solution(mesh):
    cp_size = mesh.shape['cp']
    shift_pairs = [(dev_idx, (dev_idx + 1) % cp_size) for dev_idx in range(cp_size)]

    def local_attention(x_loc, seg_loc, w_query, w_key, w_value, w_out):
        chunk_len = x_loc.shape[0]
        kv_heads = w_key.shape[1] // HEAD_DIM
        q_per_kv = w_query.shape[1] // w_key.shape[1]
        cp_rank = lax.axis_index('cp')
        q_loc = jnp.dot(x_loc, w_query, preferred_element_type=jnp.float32).astype(jnp.bfloat16).reshape(chunk_len, kv_heads, q_per_kv, HEAD_DIM)
        k_loc = jnp.dot(x_loc, w_key, preferred_element_type=jnp.float32).astype(jnp.bfloat16).reshape(chunk_len, kv_heads, HEAD_DIM)
        v_loc = jnp.dot(x_loc, w_value, preferred_element_type=jnp.float32).astype(jnp.bfloat16).reshape(chunk_len, kv_heads, HEAD_DIM)
        q_pos = cp_rank * chunk_len + jnp.arange(chunk_len)

        def visit_block(soft_state, k_blk, v_blk, seg_kv, src_chunk):
            k_pos = src_chunk * chunk_len + jnp.arange(chunk_len)
            active = (src_chunk <= cp_rank) & (seg_kv[chunk_len - 1] >= seg_loc[0])
            allowed = (seg_loc[:, None] == seg_kv[None, :]) & (q_pos[:, None] >= k_pos[None, :])
            return lax.cond(active, lambda same_state: block_update(same_state, q_loc, k_blk, v_blk, allowed), lambda same_state: same_state, soft_state)

        init_state = (jnp.full((chunk_len, kv_heads, q_per_kv), -jnp.inf, jnp.float32), jnp.zeros((chunk_len, kv_heads, q_per_kv), jnp.float32), jnp.zeros((chunk_len, kv_heads, q_per_kv, HEAD_DIM), jnp.float32))
        soft_state = visit_block(init_state, k_loc, v_loc, seg_loc, cp_rank)

        def shift_step(step_idx, loop_state):
            soft_state, k_blk, v_blk, seg_kv = loop_state
            k_blk = lax.ppermute(k_blk, 'cp', shift_pairs)
            v_blk = lax.ppermute(v_blk, 'cp', shift_pairs)
            seg_kv = lax.ppermute(seg_kv, 'cp', shift_pairs)
            src_chunk = (cp_rank - step_idx) % cp_size
            soft_state = visit_block(soft_state, k_blk, v_blk, seg_kv, src_chunk)
            return soft_state, k_blk, v_blk, seg_kv

        soft_state = lax.fori_loop(1, cp_size, shift_step, (soft_state, k_loc, v_loc, seg_loc))[0]
        heads_out = (soft_state[2] / soft_state[1][..., None]).astype(jnp.bfloat16).reshape(chunk_len, kv_heads * q_per_kv * HEAD_DIM)
        part_out = jnp.dot(heads_out, w_out, preferred_element_type=jnp.float32)
        return lax.psum(part_out, 'tp').astype(jnp.bfloat16)

    return jax.shard_map(local_attention, mesh=mesh, in_specs=(P(('dp', 'cp'), None), P(('dp', 'cp')), P(None, 'tp'), P(None, 'tp'), P(None, 'tp'), P('tp', None)), out_specs=P(('dp', 'cp'), None), check_vma=False)
```

profile of v0, /device:TPU:97, one launch (start us, length us, event | category | flops | bytes accessed | tf_op | source)
XLA Modules:
  0.0 349.6 jit_solution(12216309477892261185)
XLA Ops:
  0.0 1.5 fusion.30
  2.9 0.7 copy.56
  3.6 4.0 %convolution_convert_fusion.2 = bf16[512,256]{0,1:T(8,128)(2,1)S(1)} fusion(bf16[512,5120]{1,0:T(8,128)(2,1)} %param.12, bf16[5120,256]{1,0:T(8,128)(2,1)S(1)} %copy-done), kind=kOutput, calls=%fused_computation.43 | convolution fusion | flops 1342308352 | bytes 8126464 | tf_op jit(solution)/shard_map/dot_general | solution.py:32
  7.8 5.6 %convolution_convert_fusion.1 = bf16[512,256]{0,1:T(8,128)(2,1)} fusion(bf16[512,5120]{1,0:T(8,128)(2,1)} %param.12, bf16[5120,256]{1,0:T(8,128)(2,1)} %param.16), kind=kOutput, calls=%fused_computation.42 | convolution fusion | flops 1342308352 | bytes 8126464 | tf_op jit(solution)/shard_map/dot_general | solution.py:33
  13.4 1.1 copy.21
  14.5 9.9 %convolution_convert_fusion = bf16[512,1024]{1,0:T(8,128)(2,1)S(1)} fusion(bf16[512,5120]{1,0:T(8,128)(2,1)} %param.12, bf16[5120,1024]{1,0:T(8,128)(2,1)} %param.14), kind=kOutput, calls=%fused_computation.41 | convolution fusion | flops 5369233408 | bytes 16777216 | tf_op jit(solution)/shard_map/dot_general | solution.py:31
  24.4 0.8 reshape.38
  25.4 10.3 %conditional.2 = (f32[512,2,4]{0,2,1:T(4,128)}, f32[512,2,4]{0,2,1:T(4,128)S(1)}, f32[512,2,4,128]{3,0,2,1:T(8,128)S(1)}) conditional(s32[]{:T(128)} %bitcast.13, () %tuple.47, (s32[512]{0:T(512)S(1)}, s32[]{:T(128)}, s32[512,1]{0,1:T(1,128)S(1)}, s32[1,512]{1,0:T(1,128)S(1)}, bf16[512,2,128]{0,2,1:T(8,128)(2,1)S(1)}, ...), branch_computations={%region_0.0_spmd, %region_1.4_spmd} | conditional | flops 1098142720 | bytes 30079008 | solution.py:40
  25.7 2.7 fusion.4
  28.4 0.7 compare_select_fusion
  29.1 1.8 fusion.3
  30.8 0.7 exponential_multiply_fusion
  31.6 3.9 %bitcast_add_fusion = f32[512,2,4,128]{3,0,2,1:T(8,128)S(1)} fusion(f32[2,512,512,4]{2,1,3,0:T(8,128)S(1)} %get-tuple-element.502, f32[512,2,4]{0,2,1:T(4,128)S(1)} %compare_select_fusion, pred[512,512]{0,1:T(8,128)(4,1)S(1)} %compare_and_fusion, f32[512,2,4]{0,2,1:T(4,128)S(1)} %get-tuple-element.499, bf16[512,2,128]{0,2,1:T(8,128)(2,1)} %get-tuple-element.458), kind=kOutput, calls=%fused_computation.8 | convolution fusion | flops 545783808 | bytes 11042816 | tf_op jit(solution)/shard_map/cond/branch_1_fun/qhgk,khd->qhgd/dot_general | solution.py:18
  35.7 1.3 copy-done.2
  37.0 118.4 %while.26 = (s32[]{:T(128)}, f32[512,2,4]{0,2,1:T(4,128)}, f32[512,2,4]{0,2,1:T(4,128)S(1)}, f32[512,2,4,128]{3,0,2,1:T(8,128)}, bf16[512,2,128]{2,0,1:T(8,128)(...) while((s32[]{:T(128)}, f32[512,2,4]{0,2,1:T(4,128)}, ...), condition=%wide.region_9.10_spmd.clone, body=%wide.region_4.9_spmd.clone.sunk | while | flops 1098671104 | bytes 52216460 | solution.py:54
  37.0 2.7 collective-permute-start.2
  39.6 1.7 collective-permute-start
  41.9 3.8 %collective-permute-done = s32[512]{0:T(512)S(1)} collective-permute-done((s32[512]{0:T(512)S(1)}, s32[512]{0:T(512)S(1)}, u32[]{:S(2)}, u32[]{:S(2)}) %collective-permute-start) | collective-permute-done | bytes 2080 | tf_op jit(solution)/shard_map/while/body/eval_jaxpr/ppermute | solution.py:49
  45.8 0.6 slice.34
  47.7 10.1 %conditional.5 = ((f32[512,2,4]{0,2,1:T(4,128)}, f32[512,2,4]{0,2,1:T(4,128)S(1)}, f32[512,2,4,128]{3,0,2,1:T(8,128)})) conditional(s32[]{:T(128)} %convert_element_type.60, (f32[512,2,4]{0,2,1:T(4,128)}, f32[512,2,4]{0,2,1:T(4,128)S(1)}, f32[512,2,4,128]{3,0,2,1:T(8,128)}) %tuple.75, (s32[512]{0:T(512)S(1)}, s32[512]{0:T(512)S(1)}, s32[]{:T(128)}, ...), branch_computations={%region_5.5_spmd, %region_6.8_spmd} | conditional | flops 1098671104 | bytes 49053804 | solution.py:40
  48.1 1.4 fusion.19
  49.5 0.7 compare_select_fusion.1
  50.2 1.8 fusion.18
  52.0 0.7 multiply_add_fusion
  53.3 3.2 bitcast_add_fusion.1
  56.5 1.3 copy-done.4
  57.9 2.5 collective-permute-start.2
  60.5 1.7 collective-permute-start
  62.7 3.8 %collective-permute-done = s32[512]{0:T(512)S(1)} collective-permute-done((s32[512]{0:T(512)S(1)}, s32[512]{0:T(512)S(1)}, u32[]{:S(2)}, u32[]{:S(2)}) %collective-permute-start) | collective-permute-done | bytes 2080 | tf_op jit(solution)/shard_map/while/body/eval_jaxpr/ppermute | solution.py:49
  66.5 0.6 slice.34
  68.6 12.6 %collective-permute-start.2 = (bf16[512,2,128]{2,0,1:T(8,128)(2,1)S(1)}, bf16[512,2,128]{2,0,1:T(8,128)(2,1)S(1)}, u32[]{:S(2)}, u32[]{:S(2)}) collective-permute-start(bf16[512,2,128]{2,0,1:T(8,128)(2,1)S(1)} %get-tuple-element.612), channel_id=1, source_target_pairs={{0,1},{1,2},{2,3},{3,4},{4,5},{5,6},{6,7},{7,0},{8,9},{9,10},{10,1... | collective-permute-start | bytes 786440 | tf_op jit(solution)/shard_map/while/body/eval_jaxpr/ppermute | solution.py:48
  81.3 1.7 collective-permute-start
  83.5 3.8 %collective-permute-done = s32[512]{0:T(512)S(1)} collective-permute-done((s32[512]{0:T(512)S(1)}, s32[512]{0:T(512)S(1)}, u32[]{:S(2)}, u32[]{:S(2)}) %collective-permute-start) | collective-permute-done | bytes 2080 | tf_op jit(solution)/shard_map/while/body/eval_jaxpr/ppermute | solution.py:49
  89.4 2.5 collective-permute-start.2
  91.9 9.3 %collective-permute-start.1 = (bf16[512,2,128]{2,0,1:T(8,128)(2,1)S(1)}, bf16[512,2,128]{2,0,1:T(8,128)(2,1)S(1)}, u32[]{:S(2)}, u32[]{:S(2)}) collective-permute-start(bf16[512,2,128]{2,0,1:T(8,128)(2,1)S(1)} %get-tuple-element.611), channel_id=1, source_target_pairs={{0,1},{1,2},{2,3},{3,4},{4,5},{5,6},{6,7},{7,0},{8,9},{9,10},{10,1... | collective-permute-start | bytes 786440 | tf_op jit(solution)/shard_map/while/body/eval_jaxpr/ppermute | solution.py:47
  101.2 2.5 collective-permute-start
  106.6 2.5 collective-permute-start.2
  109.1 2.8 collective-permute-start.1
  112.0 12.6 %collective-permute-start = (s32[512]{0:T(512)S(1)}, s32[512]{0:T(512)S(1)}, u32[]{:S(2)}, u32[]{:S(2)}) collective-permute-start(s32[512]{0:T(512)S(1)} %get-tuple-element.613), channel_id=1, source_target_pairs={{0,1},{1,2},{2,3},{3,4},{4,5},{5,6},{6,7},{7,0},{8,9},{9,10},{10,1... | collective-permute-start | bytes 6152 | tf_op jit(solution)/shard_map/while/body/eval_jaxpr/ppermute | solution.py:49
  127.3 2.3 collective-permute-start.2
  129.6 3.1 collective-permute-start.1
  132.7 2.5 collective-permute-start
  138.1 9.0 %collective-permute-start.2 = (bf16[512,2,128]{2,0,1:T(8,128)(2,1)S(1)}, bf16[512,2,128]{2,0,1:T(8,128)(2,1)S(1)}, u32[]{:S(2)}, u32[]{:S(2)}) collective-permute-start(bf16[512,2,128]{2,0,1:T(8,128)(2,1)S(1)} %get-tuple-element.612), channel_id=1, source_target_pairs={{0,1},{1,2},{2,3},{3,4},{4,5},{5,6},{6,7},{7,0},{8,9},{9,10},{10,1... | collective-permute-start | bytes 786440 | tf_op jit(solution)/shard_map/while/body/eval_jaxpr/ppermute | solution.py:48
  147.2 2.5 collective-permute-start.1
  149.7 2.5 collective-permute-start
  155.3 1.9 copy.23
  157.6 12.4 %fusion.31 = f32[512,5120]{1,0:T(8,128)} fusion(bf16[512,1024]{0,1:T(8,128)(2,1)S(1)} %bitcast.69, bf16[1024,5120]{1,0:T(8,128)(2,1)} %param.17), kind=kOutput, calls=%fused_computation.45 | convolution fusion | flops 5368709120 | bytes 22020096 | tf_op jit(solution)/shard_map/dot_general | solution.py:56
  170.0 179.6 %all-reduce.1 = bf16[512,5120]{1,0:T(8,128)(2,1)} all-reduce(f32[512,5120]{1,0:T(8,128)} %fusion.31), channel_id=1, replica_groups=mesh['dp'=1,'tp'=4,'cp'=8] {'tp'}, use_global_device_ids=true, to_apply=%region_10.11 | all-reduce | flops 2621440 | bytes 15728640 | tf_op jit(solution)/shard_map/psum | solution.py:57
  (96 shorter events, 10.8 us)
Async XLA Ops:
  0.0 3.6 %copy-start = (bf16[5120,256]{1,0:T(8,128)(2,1)S(1)}, bf16[5120,256]{1,0:T(8,128)(2,1)}, u32[]{:S(2)}) copy-start(bf16[5120,256]{1,0:T(8,128)(2,1)} %param.15) | copy-start | bytes 7864324
  14.5 10.7 %copy-start.5 = (s32[512]{0:T(512)S(1)}, s32[512]{0:T(512)}, u32[]{:S(2)}) copy-start(s32[512]{0:T(512)} %param.13) | copy-start | bytes 6148
  35.6 1.3 copy-start.2
  37.0 10.7 %collective-permute-start.2 = (bf16[512,2,128]{2,0,1:T(8,128)(2,1)S(1)}, bf16[512,2,128]{2,0,1:T(8,128)(2,1)S(1)}, u32[]{:S(2)}, u32[]{:S(2)}) collective-permute-start(bf16[512,2,128]{2,0,1:T(8,128)(2,1)S(1)} %get-tuple-element.612), channel_id=1, source_target_pairs={{0,1},{1,2},{2,3},{3,4},{4,5},{5,6},{6,7},{7,0},{8,9},{9,10},{10,1... | collective-permute-start | bytes 786440 | tf_op jit(solution)/shard_map/while/body/eval_jaxpr/ppermute | solution.py:48
  39.6 8.1 %collective-permute-start.1 = (bf16[512,2,128]{2,0,1:T(8,128)(2,1)S(1)}, bf16[512,2,128]{2,0,1:T(8,128)(2,1)S(1)}, u32[]{:S(2)}, u32[]{:S(2)}) collective-permute-start(bf16[512,2,128]{2,0,1:T(8,128)(2,1)S(1)} %get-tuple-element.611), channel_id=1, source_target_pairs={{0,1},{1,2},{2,3},{3,4},{4,5},{5,6},{6,7},{7,0},{8,9},{9,10},{10,1... | collective-permute-start | bytes 786440 | tf_op jit(solution)/shard_map/while/body/eval_jaxpr/ppermute | solution.py:47
  39.6 6.1 %collective-permute-start = (s32[512]{0:T(512)S(1)}, s32[512]{0:T(512)S(1)}, u32[]{:S(2)}, u32[]{:S(2)}) collective-permute-start(s32[512]{0:T(512)S(1)} %get-tuple-element.613), channel_id=1, source_target_pairs={{0,1},{1,2},{2,3},{3,4},{4,5},{5,6},{6,7},{7,0},{8,9},{9,10},{10,1... | collective-permute-start | bytes 6152 | tf_op jit(solution)/shard_map/while/body/eval_jaxpr/ppermute | solution.py:49
  48.0 5.3 %copy-start.3 = (f32[512,2,4,128]{3,0,2,1:T(8,128)S(1)}, f32[512,2,4,128]{3,0,2,1:T(8,128)}, u32[]{:S(2)}) copy-start(f32[512,2,4,128]{3,0,2,1:T(8,128)} %get-tuple-element.379) | copy-start | bytes 6291460 | tf_op jit(solution)/shard_map/while/body/eval_jaxpr/cond
  56.5 1.3 copy-start.4
  57.9 10.6 %collective-permute-start.2 = (bf16[512,2,128]{2,0,1:T(8,128)(2,1)S(1)}, bf16[512,2,128]{2,0,1:T(8,128)(2,1)S(1)}, u32[]{:S(2)}, u32[]{:S(2)}) collective-permute-start(bf16[512,2,128]{2,0,1:T(8,128)(2,1)S(1)} %get-tuple-element.612), channel_id=1, source_target_pairs={{0,1},{1,2},{2,3},{3,4},{4,5},{5,6},{6,7},{7,0},{8,9},{9,10},{10,1... | collective-permute-start | bytes 786440 | tf_op jit(solution)/shard_map/while/body/eval_jaxpr/ppermute | solution.py:48
  60.4 8.1 %collective-permute-start.1 = (bf16[512,2,128]{2,0,1:T(8,128)(2,1)S(1)}, bf16[512,2,128]{2,0,1:T(8,128)(2,1)S(1)}, u32[]{:S(2)}, u32[]{:S(2)}) collective-permute-start(bf16[512,2,128]{2,0,1:T(8,128)(2,1)S(1)} %get-tuple-element.611), channel_id=1, source_target_pairs={{0,1},{1,2},{2,3},{3,4},{4,5},{5,6},{6,7},{7,0},{8,9},{9,10},{10,1... | collective-permute-start | bytes 786440 | tf_op jit(solution)/shard_map/while/body/eval_jaxpr/ppermute | solution.py:47
  60.5 6.1 %collective-permute-start = (s32[512]{0:T(512)S(1)}, s32[512]{0:T(512)S(1)}, u32[]{:S(2)}, u32[]{:S(2)}) collective-permute-start(s32[512]{0:T(512)S(1)} %get-tuple-element.613), channel_id=1, source_target_pairs={{0,1},{1,2},{2,3},{3,4},{4,5},{5,6},{6,7},{7,0},{8,9},{9,10},{10,1... | collective-permute-start | bytes 6152 | tf_op jit(solution)/shard_map/while/body/eval_jaxpr/ppermute | solution.py:49
  68.6 20.6 %collective-permute-start.2 = (bf16[512,2,128]{2,0,1:T(8,128)(2,1)S(1)}, bf16[512,2,128]{2,0,1:T(8,128)(2,1)S(1)}, u32[]{:S(2)}, u32[]{:S(2)}) collective-permute-start(bf16[512,2,128]{2,0,1:T(8,128)(2,1)S(1)} %get-tuple-element.612), channel_id=1, source_target_pairs={{0,1},{1,2},{2,3},{3,4},{4,5},{5,6},{6,7},{7,0},{8,9},{9,10},{10,1... | collective-permute-start | bytes 786440 | tf_op jit(solution)/shard_map/while/body/eval_jaxpr/ppermute | solution.py:48
  81.2 8.1 %collective-permute-start.1 = (bf16[512,2,128]{2,0,1:T(8,128)(2,1)S(1)}, bf16[512,2,128]{2,0,1:T(8,128)(2,1)S(1)}, u32[]{:S(2)}, u32[]{:S(2)}) collective-permute-start(bf16[512,2,128]{2,0,1:T(8,128)(2,1)S(1)} %get-tuple-element.611), channel_id=1, source_target_pairs={{0,1},{1,2},{2,3},{3,4},{4,5},{5,6},{6,7},{7,0},{8,9},{9,10},{10,1... | collective-permute-start | bytes 786440 | tf_op jit(solution)/shard_map/while/body/eval_jaxpr/ppermute | solution.py:47
  81.3 6.1 %collective-permute-start = (s32[512]{0:T(512)S(1)}, s32[512]{0:T(512)S(1)}, u32[]{:S(2)}, u32[]{:S(2)}) collective-permute-start(s32[512]{0:T(512)S(1)} %get-tuple-element.613), channel_id=1, source_target_pairs={{0,1},{1,2},{2,3},{3,4},{4,5},{5,6},{6,7},{7,0},{8,9},{9,10},{10,1... | collective-permute-start | bytes 6152 | tf_op jit(solution)/shard_map/while/body/eval_jaxpr/ppermute | solution.py:49
  89.4 17.1 %collective-permute-start.2 = (bf16[512,2,128]{2,0,1:T(8,128)(2,1)S(1)}, bf16[512,2,128]{2,0,1:T(8,128)(2,1)S(1)}, u32[]{:S(2)}, u32[]{:S(2)}) collective-permute-start(bf16[512,2,128]{2,0,1:T(8,128)(2,1)S(1)} %get-tuple-element.612), channel_id=1, source_target_pairs={{0,1},{1,2},{2,3},{3,4},{4,5},{5,6},{6,7},{7,0},{8,9},{9,10},{10,1... | collective-permute-start | bytes 786440 | tf_op jit(solution)/shard_map/while/body/eval_jaxpr/ppermute | solution.py:48
  91.9 14.5 %collective-permute-start.1 = (bf16[512,2,128]{2,0,1:T(8,128)(2,1)S(1)}, bf16[512,2,128]{2,0,1:T(8,128)(2,1)S(1)}, u32[]{:S(2)}, u32[]{:S(2)}) collective-permute-start(bf16[512,2,128]{2,0,1:T(8,128)(2,1)S(1)} %get-tuple-element.611), channel_id=1, source_target_pairs={{0,1},{1,2},{2,3},{3,4},{4,5},{5,6},{6,7},{7,0},{8,9},{9,10},{10,1... | collective-permute-start | bytes 786440 | tf_op jit(solution)/shard_map/while/body/eval_jaxpr/ppermute | solution.py:47
  101.2 3.3 collective-permute-start
  106.6 20.6 %collective-permute-start.2 = (bf16[512,2,128]{2,0,1:T(8,128)(2,1)S(1)}, bf16[512,2,128]{2,0,1:T(8,128)(2,1)S(1)}, u32[]{:S(2)}, u32[]{:S(2)}) collective-permute-start(bf16[512,2,128]{2,0,1:T(8,128)(2,1)S(1)} %get-tuple-element.612), channel_id=1, source_target_pairs={{0,1},{1,2},{2,3},{3,4},{4,5},{5,6},{6,7},{7,0},{8,9},{9,10},{10,1... | collective-permute-start | bytes 786440 | tf_op jit(solution)/shard_map/while/body/eval_jaxpr/ppermute | solution.py:48
  109.1 18.0 %collective-permute-start.1 = (bf16[512,2,128]{2,0,1:T(8,128)(2,1)S(1)}, bf16[512,2,128]{2,0,1:T(8,128)(2,1)S(1)}, u32[]{:S(2)}, u32[]{:S(2)}) collective-permute-start(bf16[512,2,128]{2,0,1:T(8,128)(2,1)S(1)} %get-tuple-element.611), channel_id=1, source_target_pairs={{0,1},{1,2},{2,3},{3,4},{4,5},{5,6},{6,7},{7,0},{8,9},{9,10},{10,1... | collective-permute-start | bytes 786440 | tf_op jit(solution)/shard_map/while/body/eval_jaxpr/ppermute | solution.py:47
  112.0 13.3 %collective-permute-start = (s32[512]{0:T(512)S(1)}, s32[512]{0:T(512)S(1)}, u32[]{:S(2)}, u32[]{:S(2)}) collective-permute-start(s32[512]{0:T(512)S(1)} %get-tuple-element.613), channel_id=1, source_target_pairs={{0,1},{1,2},{2,3},{3,4},{4,5},{5,6},{6,7},{7,0},{8,9},{9,10},{10,1... | collective-permute-start | bytes 6152 | tf_op jit(solution)/shard_map/while/body/eval_jaxpr/ppermute | solution.py:49
  127.3 10.7 %collective-permute-start.2 = (bf16[512,2,128]{2,0,1:T(8,128)(2,1)S(1)}, bf16[512,2,128]{2,0,1:T(8,128)(2,1)S(1)}, u32[]{:S(2)}, u32[]{:S(2)}) collective-permute-start(bf16[512,2,128]{2,0,1:T(8,128)(2,1)S(1)} %get-tuple-element.612), channel_id=1, source_target_pairs={{0,1},{1,2},{2,3},{3,4},{4,5},{5,6},{6,7},{7,0},{8,9},{9,10},{10,1... | collective-permute-start | bytes 786440 | tf_op jit(solution)/shard_map/while/body/eval_jaxpr/ppermute | solution.py:48
  129.6 8.4 %collective-permute-start.1 = (bf16[512,2,128]{2,0,1:T(8,128)(2,1)S(1)}, bf16[512,2,128]{2,0,1:T(8,128)(2,1)S(1)}, u32[]{:S(2)}, u32[]{:S(2)}) collective-permute-start(bf16[512,2,128]{2,0,1:T(8,128)(2,1)S(1)} %get-tuple-element.611), channel_id=1, source_target_pairs={{0,1},{1,2},{2,3},{3,4},{4,5},{5,6},{6,7},{7,0},{8,9},{9,10},{10,1... | collective-permute-start | bytes 786440 | tf_op jit(solution)/shard_map/while/body/eval_jaxpr/ppermute | solution.py:47
  132.7 3.3 collective-permute-start
  138.1 17.1 %collective-permute-start.2 = (bf16[512,2,128]{2,0,1:T(8,128)(2,1)S(1)}, bf16[512,2,128]{2,0,1:T(8,128)(2,1)S(1)}, u32[]{:S(2)}, u32[]{:S(2)}) collective-permute-start(bf16[512,2,128]{2,0,1:T(8,128)(2,1)S(1)} %get-tuple-element.612), channel_id=1, source_target_pairs={{0,1},{1,2},{2,3},{3,4},{4,5},{5,6},{6,7},{7,0},{8,9},{9,10},{10,1... | collective-permute-start | bytes 786440 | tf_op jit(solution)/shard_map/while/body/eval_jaxpr/ppermute | solution.py:48
  147.2 8.1 %collective-permute-start.1 = (bf16[512,2,128]{2,0,1:T(8,128)(2,1)S(1)}, bf16[512,2,128]{2,0,1:T(8,128)(2,1)S(1)}, u32[]{:S(2)}, u32[]{:S(2)}) collective-permute-start(bf16[512,2,128]{2,0,1:T(8,128)(2,1)S(1)} %get-tuple-element.611), channel_id=1, source_target_pairs={{0,1},{1,2},{2,3},{3,4},{4,5},{5,6},{6,7},{7,0},{8,9},{9,10},{10,1... | collective-permute-start | bytes 786440 | tf_op jit(solution)/shard_map/while/body/eval_jaxpr/ppermute | solution.py:47
  149.7 3.6 %collective-permute-start = (s32[512]{0:T(512)S(1)}, s32[512]{0:T(512)S(1)}, u32[]{:S(2)}, u32[]{:S(2)}) collective-permute-start(s32[512]{0:T(512)S(1)} %get-tuple-element.613), channel_id=1, source_target_pairs={{0,1},{1,2},{2,3},{3,4},{4,5},{5,6},{6,7},{7,0},{8,9},{9,10},{10,1... | collective-permute-start | bytes 6152 | tf_op jit(solution)/shard_map/while/body/eval_jaxpr/ppermute | solution.py:49
  157.6 192.0 %copy-start.1 = (bf16[5120,256]{1,0:T(8,128)(2,1)S(1)}, bf16[5120,256]{1,0:T(8,128)(2,1)}, u32[]{:S(2)}) copy-start(bf16[5120,256]{1,0:T(8,128)(2,1)} %param.15) | copy-start | bytes 7864324
where the time goes:
time: 356 us; the launch traced here: 350 us
  blocking collectives  180 us (51%)
  starting transfers between devices  77.2 us (22%)
  matrix products  43.1 us (12%)
  local copies, waits for them, and re-layouts  18.2 us (5%)
  waiting for transfers between devices  12.9 us (4%)
  loops' own time  9.81 us (3%)
  other arithmetic  7.3 us (2%)
    psum x1, blocking collectives, local_attention(): return lax.psum(part_out, 'tp').astype(jnp.bfloat16)  180 us
    ppermute x7, starting transfers between devices, shift_step(): v_blk = lax.ppermute(v_blk, 'cp', shift_pairs)  34.3 us
    ppermute x7, starting transfers between devices, shift_step(): seg_kv = lax.ppermute(seg_kv, 'cp', shift_pairs)  25.1 us
    ppermute x7, starting transfers between devices, shift_step(): k_blk = lax.ppermute(k_blk, 'cp', shift_pairs)  17.9 us
    ppermute x7, waiting for transfers between devices, shift_step(): seg_kv = lax.ppermute(seg_kv, 'cp', shift_pairs)  12.9 us
    dot_general x1, matrix products, local_attention(): part_out = jnp.dot(heads_out, w_out, preferred_element_type=jnp.float32)  12.4 us
    dot_general x1, matrix products, local_attention(): jnp.dot(x_loc, w_query, preferred_element_type=jnp.float32)  9.92 us
    slice x15, local copies, waits for them, and re-layouts, visit_block(): active = (src_chunk <= cp_rank) & (seg_kv[chunk_len - 1] >= seg_loc[0])  9.76 us
  transfers between devices with their start and end apart: 21, of which 7 were waited for; matrix products, arithmetic and copies ran while one was open for 2% of the time, Pallas kernels for 0%

commit v1 on v0

v1 whole, which is shorter than its diff:
```python
import functools

import jax
import jax.numpy as jnp
from jax import lax
from jax.experimental import pallas as pl
from jax.experimental.pallas import tpu as pltpu
from jax.sharding import PartitionSpec as P

HEAD_DIM = 128
COL_TILE = 256
MESH = pl.DeviceIdType.MESH
SCALE = HEAD_DIM**-0.5 * 1.4426950408889634
NEG_INF = float("-inf")


class Sems:
    def __init__(self, ref):
        self.ref, self.names = ref, {}

    def __getitem__(self, name):
        return self.ref.at[self.names.setdefault(name, len(self.names))]


def kernel(tp, cp, x_hbm, seg_in, wq_hbm, wk_hbm, wv_hbm, wo_hbm, y_hbm,
           x_v, wkv_v, wq_v, w_full, kv_all, segs, seg_col, q_v, o_all, y_own, relay_up, relay_dn,
           m_s, l_s, acc_s, load_sem, send_sem, recv_sem):
    t, p = lax.axis_index("tp"), lax.axis_index("cp")
    chips = cp // 2
    col, core = p // 2, lax.rem(p, 2)
    up, dn, far = lax.rem(t + 1, tp), lax.rem(t + tp - 1, tp), lax.rem(t + 2, tp)
    right_chip, left_chip, far_chip = lax.rem(col + 1, chips), lax.rem(col + chips - 1, chips), lax.rem(col + 2, chips)
    right, left, across = right_chip * 2 + core, left_chip * 2 + core, far_chip * 2 + core
    mate = col * 2 + 1 - core
    mate_right, mate_left, mate_across = right_chip * 2 + 1 - core, left_chip * 2 + 1 - core, far_chip * 2 + 1 - core

    rows = x_v.shape[0]
    heads = q_v.shape[0]
    groups = kv_all.shape[1]
    per_group = heads // groups
    head_cols = heads * HEAD_DIM
    y_cols = y_own.shape[1]
    piece = head_cols // cp
    half = piece // 2
    half_rows = rows // 2

    loads, sends, recvs = Sems(load_sem), Sems(send_sem), Sems(recv_sem)
    waiting = []

    def at_tp(i):
        return {"tp": i, "cp": p}

    def at_cp(i):
        return {"tp": t, "cp": i}

    def send(src, dst, name, dev):
        c = pltpu.make_async_remote_copy(src_ref=src, dst_ref=dst, send_sem=sends[(name, len(waiting))],
                                         recv_sem=recvs[name], device_id=dev, device_id_type=MESH)
        c.start()
        waiting.append(c)

    def arrived(dst, name):
        pltpu.make_async_remote_copy(src_ref=dst, dst_ref=dst, send_sem=sends[0], recv_sem=recvs[name],
                                     device_id=at_cp(p), device_id_type=MESH).wait_recv()

    def load(src, dst, name):
        c = pltpu.make_async_copy(src, dst, loads[name])
        c.start()
        return c

    load_x = load(x_hbm, x_v, "x")
    load_k = load(wk_hbm, wkv_v.at[0], "k")
    load_v = load(wv_hbm, wkv_v.at[1], "v")
    q_tiles = head_cols // COL_TILE
    load_q = [load(wq_hbm.at[:, pl.ds(n * COL_TILE, COL_TILE)], wq_v.at[n], ("q", n)) for n in range(q_tiles)]
    own_cols = pl.ds(pl.multiple_of(t * y_cols, 128), y_cols)
    load_o = load(wo_hbm.at[:, own_cols], w_full.at[pl.ds(pl.multiple_of(t * head_cols, 128), head_cols), :], "o")

    barrier = pltpu.get_barrier_semaphore()
    peers = [at_tp(up), at_tp(dn)] + [at_cp(lax.rem(p + k, cp)) for k in range(1, cp)]
    for dev in peers:
        pl.semaphore_signal(barrier, inc=1, device_id=dev, device_id_type=MESH)
    pl.semaphore_wait(barrier, len(peers))

    for k in range(1, cp):
        send(seg_in, segs.at[p], ("seg", k), at_cp(lax.rem(p + k, cp)))
    load_seg = load(seg_in, segs.at[p], "seg")

    def w_rows(owner, share, k=None):
        start = owner * head_cols + share * piece
        if k is None:
            return w_full.at[pl.ds(pl.multiple_of(start, 16), piece), :]
        return w_full.at[pl.ds(pl.multiple_of(start + k * half, 16), half), :]

    def w_src(dest, k=None):
        cols = pl.ds(pl.multiple_of(dest * y_cols, 128), y_cols)
        if k is None:
            return wo_hbm.at[pl.ds(pl.multiple_of(p * piece, 16), piece), cols]
        return wo_hbm.at[pl.ds(pl.multiple_of(p * piece + k * half, 16), half), cols]

    send(w_src(far, 0), relay_up, "w_relay_up", at_tp(up))
    send(w_src(far, 1), relay_dn, "w_relay_dn", at_tp(dn))
    send(w_src(up), w_rows(t, p), "w_from_dn", at_tp(up))
    send(w_src(dn), w_rows(t, p), "w_from_up", at_tp(dn))

    def ring_start(part, tag):
        send(part(p), part(p), (tag, "L"), at_cp(right))
        send(part(p), part(p), (tag, "R"), at_cp(left))
        send(part(p), part(p), (tag, "M"), at_cp(mate))

    def ring_near(part, tag):
        arrived(part(left), (tag, "L"))
        send(part(left, 0), part(left, 0), (tag, "far0"), at_cp(right))
        send(part(left), part(left), (tag, "ML"), at_cp(mate))
        arrived(part(right), (tag, "R"))
        send(part(right, 1), part(right, 1), (tag, "far1"), at_cp(left))
        send(part(right), part(right), (tag, "MR"), at_cp(mate))

    def ring_far(part, tag):
        arrived(part(across, 0), (tag, "far0"))
        arrived(part(across, 1), (tag, "far1"))
        send(part(across), part(across), (tag, "MF"), at_cp(mate))

    def kv_part(g):
        return lambda owner, k=None: kv_all.at[owner, g] if k is None else kv_all.at[owner, g, k]

    def project(w_ref, store):
        @pl.loop(0, rows // half_rows)
        def _(i):
            r = pl.ds(pl.multiple_of(i * half_rows, 16), half_rows)
            store(r, jnp.dot(x_v[r, :], w_ref[...], preferred_element_type=jnp.float32).astype(jnp.bfloat16))

    load_x.wait()
    load_k.wait()

    def store_k(kind):
        def store(r, val):
            for g in range(groups):
                kv_all[p, g, kind, r, :] = val[:, g * HEAD_DIM:(g + 1) * HEAD_DIM]
        return store

    project(wkv_v.at[0], store_k(0))
    load_v.wait()
    project(wkv_v.at[1], store_k(1))
    ring_start(kv_part(0), ("kv", 0))

    def q_tile(n):
        load_q[n].wait()

        def store(r, val):
            for k in range(COL_TILE // HEAD_DIM):
                q_v[n * (COL_TILE // HEAD_DIM) + k, r, :] = val[:, k * HEAD_DIM:(k + 1) * HEAD_DIM]
        project(wq_v.at[n], store)

    q_tile(0)
    arrived(relay_up, "w_relay_up")
    send(relay_up, w_rows(dn, p, 0), "w_far0", at_tp(up))
    arrived(relay_dn, "w_relay_dn")
    send(relay_dn, w_rows(up, p, 1), "w_far1", at_tp(dn))
    for n in range(1, q_tiles):
        q_tile(n)

    seg_col[...] = jnp.broadcast_to(seg_in[...], (HEAD_DIM, rows)).T

    def wide(v, n):
        return jnp.concatenate([v] * (n // v.shape[1]), axis=1)

    def visit(g, block, diagonal):
        seg_k = segs[block]

        @pl.loop(0, per_group)
        def _(h):
            for i in range(2):
                r = slice(i * half_rows, (i + 1) * half_rows)
                s = lax.dot_general(q_v[g * per_group + h, r, :], kv_all[block, g, 0], (((1,), (1,)), ((), ())),
                                    preferred_element_type=jnp.float32)
                allowed = wide(seg_col[r, :], rows) == seg_k
                if diagonal:
                    allowed &= (lax.broadcasted_iota(jnp.int32, s.shape, 0) + i * half_rows
                                >= lax.broadcasted_iota(jnp.int32, s.shape, 1))
                s = jnp.where(allowed, s * SCALE, NEG_INF)
                top = jnp.max(s, axis=1, keepdims=True)
                if diagonal:
                    new_max = jnp.broadcast_to(top, (half_rows, HEAD_DIM))
                else:
                    old_max = m_s[h, r, :]
                    new_max = jnp.maximum(old_max, top)
                prob = jnp.exp2(s - wide(new_max, rows))
                part = prob[:, :HEAD_DIM]
                for k in range(1, rows // HEAD_DIM):
                    part += prob[:, k * HEAD_DIM:(k + 1) * HEAD_DIM]
                out = jnp.dot(prob.astype(jnp.bfloat16), kv_all[block, g, 1], preferred_element_type=jnp.float32)
                if not diagonal:
                    rescale = jnp.exp2(old_max - new_max)
                    part += l_s[h, r, :] * rescale
                    out += acc_s[h, r, :] * rescale
                m_s[h, r, :] = new_max
                l_s[h, r, :] = part
                acc_s[h, r, :] = out

    def visit_chip(g, first_chip, both):
        chips_here = [first_chip] if both is None else [first_chip, both]

        @pl.loop(0, 2 * len(chips_here))
        def _(i):
            chip = chips_here[0] if both is None else jnp.where(i < 2, chips_here[0], chips_here[1])
            block = chip * 2 + lax.rem(i, 2)

            @pl.when(block < p)
            def _():
                visit(g, block, False)

    def o_cols(owner, h):
        return o_all.at[:, pl.ds(pl.multiple_of(owner * head_cols + h * HEAD_DIM, 128), HEAD_DIM)]

    def o_relay(h):
        arrived(o_cols(dn, h), ("o", h, "D"))
        arrived(o_cols(up, h), ("o", h, "U"))
        if h % 2 == 0:
            send(o_cols(dn, h), o_cols(dn, h), ("o", h, "F"), at_tp(up))
        else:
            send(o_cols(up, h), o_cols(up, h), ("o", h, "F"), at_tp(dn))

    load_seg.wait()
    for k in range(1, cp):
        arrived(segs.at[lax.rem(p + cp - k, cp)], ("seg", k))

    for g in range(groups):
        part, tag = kv_part(g), ("kv", g)
        visit(g, p, True)
        ring_near(part, tag)
        if g + 1 < groups:
            ring_start(kv_part(g + 1), ("kv", g + 1))
        arrived(part(mate), (tag, "M"))
        arrived(part(mate_left), (tag, "ML"))
        arrived(part(mate_right), (tag, "MR"))

        @pl.when(core == 1)
        def _():
            visit(g, mate, False)
        visit_chip(g, left_chip, right_chip)
        ring_far(part, tag)
        arrived(part(mate_across), (tag, "MF"))
        visit_chip(g, far_chip, None)
        for k in range(per_group):
            h = g * per_group + k
            total = jnp.sum(l_s[k], axis=1, keepdims=True)
            o_all[:, pl.ds(pl.multiple_of(t * head_cols + h * HEAD_DIM, 128), HEAD_DIM)] = (
                acc_s[k] / total).astype(jnp.bfloat16)
            send(o_cols(t, h), o_cols(t, h), ("o", h, "D"), at_tp(up))
            send(o_cols(t, h), o_cols(t, h), ("o", h, "U"), at_tp(dn))
        if g == 0:
            arrived(w_rows(dn, p), "w_from_dn")
            arrived(w_rows(up, p), "w_from_up")
            arrived(w_rows(far, p, 0), "w_far0")
            arrived(w_rows(far, p, 1), "w_far1")
            for j in range(1, tp):
                ring_start(w_part(w_rows, lax.rem(t + j, tp)), ("w", j))

    w_parts = [(w_part(w_rows, lax.rem(t + j, tp)), ("w", j)) for j in range(1, tp)]
    for part, tag in w_parts:
        ring_near(part, tag)
    for h in range(heads):
        o_relay(h)
    for part, tag in w_parts:
        ring_far(part, tag)
    for part, tag in w_parts:
        arrived(part(mate), (tag, "M"))
        arrived(part(mate_left), (tag, "ML"))
        arrived(part(mate_right), (tag, "MR"))
        arrived(part(mate_across), (tag, "MF"))
    for h in range(heads):
        arrived(o_cols(far, h), ("o", h, "F"))
    load_o.wait()

    def y_at(owner, n, k=None):
        cols = pl.ds(pl.multiple_of(owner * y_cols + n * COL_TILE, 128), COL_TILE)
        return y_hbm.at[:, cols] if k is None else y_hbm.at[pl.ds(k * half_rows, half_rows), cols]

    copies = []
    tiles = y_cols // COL_TILE
    for n in range(tiles):
        c = pl.ds(n * COL_TILE, COL_TILE)

        @pl.loop(0, 2)
        def _(i):
            r = pl.ds(pl.multiple_of(i * half_rows, 16), half_rows)
            y_own[r, c] = jnp.dot(o_all[r, :], w_full[:, c], preferred_element_type=jnp.float32).astype(jnp.bfloat16)
        send(y_own.at[:, c], y_at(t, n), ("y", n, "D"), at_tp(up))
        send(y_own.at[:, c], y_at(t, n), ("y", n, "U"), at_tp(dn))
        copies.append(load(y_own.at[:, c], y_at(t, n), ("y", n)))
    for n in range(tiles):
        arrived(y_at(dn, n), ("y", n, "D"))
        send(y_at(dn, n, 0), y_at(dn, n, 0), ("y", n, "F0"), at_tp(up))
        arrived(y_at(up, n), ("y", n, "U"))
        send(y_at(up, n, 1), y_at(up, n, 1), ("y", n, "F1"), at_tp(dn))
    for n in range(tiles):
        arrived(y_at(far, n, 0), ("y", n, "F0"))
        arrived(y_at(far, n, 1), ("y", n, "F1"))
    for c in copies:
        c.wait()
    for c in waiting:
        c.wait_send()


def w_part(w_rows, owner):
    return lambda share, k=None: w_rows(owner, share, k)


def solution(mesh):
    tp, cp = mesh.shape["tp"], mesh.shape["cp"]

    def local_attention(x_loc, seg_loc, w_query, w_key, w_value, w_out):
        rows, width = x_loc.shape
        heads = w_query.shape[1] // HEAD_DIM
        groups = w_key.shape[1] // HEAD_DIM
        head_cols = heads * HEAD_DIM
        y_cols = width // tp
        bf16, f32 = jnp.bfloat16, jnp.float32
        hbm = pl.BlockSpec(memory_space=pl.ANY)
        return pl.pallas_call(
            functools.partial(kernel, tp, cp),
            out_shape=jax.ShapeDtypeStruct((rows, width), bf16),
            in_specs=[hbm, pl.BlockSpec(memory_space=pltpu.VMEM), hbm, hbm, hbm, hbm],
            out_specs=hbm,
            scratch_shapes=[
                pltpu.VMEM((rows, width), bf16),
                pltpu.VMEM((2, width, groups * HEAD_DIM), bf16),
                pltpu.VMEM((head_cols // COL_TILE, width, COL_TILE), bf16),
                pltpu.VMEM((tp * head_cols, y_cols), bf16),
                pltpu.VMEM((cp, groups, 2, rows, HEAD_DIM), bf16),
                pltpu.VMEM((cp, 1, rows), jnp.int32),
                pltpu.VMEM((rows, HEAD_DIM), jnp.int32),
                pltpu.VMEM((heads, rows, HEAD_DIM), bf16),
                pltpu.VMEM((rows, tp * head_cols), bf16),
                pltpu.VMEM((rows, y_cols), bf16),
                pltpu.VMEM((head_cols // cp // 2, y_cols), bf16),
                pltpu.VMEM((head_cols // cp // 2, y_cols), bf16),
                pltpu.VMEM((heads // groups, rows, HEAD_DIM), f32),
                pltpu.VMEM((heads // groups, rows, HEAD_DIM), f32),
                pltpu.VMEM((heads // groups, rows, HEAD_DIM), f32),
                pltpu.SemaphoreType.DMA((32,)),
                pltpu.SemaphoreType.DMA((160,)),
                pltpu.SemaphoreType.DMA((160,)),
            ],
            compiler_params=pltpu.CompilerParams(collective_id=0, has_side_effects=True, vmem_limit_bytes=67043328),
        )(x_loc, seg_loc.reshape(1, rows), w_query, w_key, w_value, w_out)

    return jax.shard_map(local_attention, mesh=mesh, in_specs=(P(('dp', 'cp'), None), P(('dp', 'cp')), P(None, 'tp'), P(None, 'tp'), P(None, 'tp'), P('tp', None)), out_specs=P(('dp', 'cp'), None), check_vma=False)
```

time: 356 us -> 157 us (0.44)
  the two profiles are of different devices: /device:TPU:97 before, /device:TPU:101 now
where the time goes in v1:
time: 157 us
  Pallas kernels  152 us (97%)
  local copies, waits for them, and re-layouts  5.18 us (3%)
    pallas_call x1, Pallas kernels, local_attention(): pl.pallas_call(functools.partial(kernel, tp, cp), out_shape=jax.ShapeDtyp...  152 us
    unnamed x1, local copies, waits for them, and re-layouts  5.18 us

profile of v1, /device:TPU:101, one launch (start us, length us, event | category | flops | bytes accessed | tf_op | source)
XLA Modules:
  0.0 157.1 jit_solution(13407840598474257249)
XLA Ops:
  0.0 151.9 %shard_map.64 = bf16[512,5120]{1,0:T(8,128)(2,1)} custom-call(bf16[512,5120]{1,0:T(8,128)(2,1)} %x_hbm.1, s32[1,512]{1,0:T(1,128)} %bitcast.1, bf16[5120,1024]{1,0:T(8,128)(2,1)} %wq_hbm.1, bf16[5120,256]{1,0:T(8,128)(2,1)} %wk_hbm.1, bf16[5120,256]{1,0:T(8,128)(2,1)} %wv_hbm.1, bf16[1024,5120]{1,0:T(8,128)(2,1)} %wo_hbm.1), custom_call_target="tpu_custom_call" | custom-call | tf_op jit(solution)/shard_map/pallas_call | solution.py:321
  151.9 5.2 %copy.8 = bf16[512,5120]{1,0:T(8,128)(2,1)} copy(bf16[512,5120]{1,0:T(8,128)(2,1)} %shard_map.64) | data formatting | bytes 10485760
